TPU v7x, 32 devices: a whole 2x2x4 slice. The times are simulated.
32 devices in a mesh: section: 4 (over y, x), stem: 8 (over z, core).
Axes of the slice: x: 2, y: 2, z: 4, core: 2. Of those that a mesh axis runs over, the one named last changes fastest.
Arguments:
- bitstrings: int32 [4, 4, 32, 3], P('section'), may hold values 0 or 1
- boundary: float32 [2, 2048], replicated, may hold values from -6 to 6
- stem_tensor: float32 [4, 2, 2048, 8, 2048], P('section', None, 'stem'), may hold values from -0.09375 to 0.09375
- probe_vectors: float32 [4, 2, 2048], P('section'), may hold values from -0.09375 to 0.09375
- inbound_permutations: int32 [4, 2048], replicated, may hold values from 0 to 2047, each once within a row
Outputs:
- amplitudes: float32 [4, 2, 4, 32], P('section')
Inputs may be any that keep to these rules, and one draw needn't show every extreme that they name: `inbound_permutations`: each row of relabeling names every number of 0 to 2047 once.
All inputs are finite; a program needn't handle non-finite values. No bound on the sum of `bitstrings` on one device may be relied on, other than what follows from the above.
Results may differ from a plain program's by a relative error of at most 0.0003.
Values sent between devices are 32-bit elements; how exact they have to be, the bound alone decides.
A program may use at most 128 MiB of HBM per device.

v0:
```python
import jax
import jax.numpy as jnp
from jax import lax
from jax.sharding import PartitionSpec as P


def from_behind(block, axis, distance):
    devices = range(lax.axis_size(axis))
    route = [(i - distance, i) for i in devices if i - distance in devices]
    return lax.ppermute(block, axis, route)


def local(bitstrings, boundary, stem_tensor, probe_vectors, inbound_permutations):
    section_count = lax.axis_size("section")
    segment_ordinal = lax.axis_index("section")
    stem_rank = lax.axis_index("stem")
    local_rows = stem_tensor.shape[2]
    settings_count = stem_tensor.shape[3]
    width = stem_tensor.shape[4]
    micro_count = bitstrings.shape[1]
    batch_size = bitstrings.shape[2]
    qubit_count = bitstrings.shape[3]
    powers = jnp.left_shift(jnp.int32(1), jnp.arange(qubit_count, dtype=jnp.int32))
    bit_patterns = jnp.sum(bitstrings[0] * powers, axis=-1)
    weight_real = stem_tensor[0, 0].reshape(local_rows * settings_count, width)
    weight_imag = stem_tensor[0, 1].reshape(local_rows * settings_count, width)
    own_perm = lax.dynamic_index_in_dim(inbound_permutations, segment_ordinal, 0, False)
    row_ids = lax.dynamic_slice_in_dim(own_perm, stem_rank * local_rows, local_rows)
    start_state = jnp.broadcast_to(
        jnp.take(boundary, row_ids, axis=1)[:, None, :], (2, batch_size, local_rows)
    )
    probe_re = probe_vectors[0, 0]
    probe_im = probe_vectors[0, 1]
    setting_ids = jnp.arange(settings_count, dtype=jnp.int32)

    def advance(moment, state_pair):
        incoming, buffer = state_pair
        position = moment - segment_ordinal
        active = jnp.logical_and(position >= 0, position < micro_count)
        clipped = jnp.clip(position, 0, micro_count - 1)
        pattern = lax.dynamic_index_in_dim(bit_patterns, clipped, 0, False)
        gathered = lax.all_gather(incoming, "stem", axis=2, tiled=True)
        arriving = jnp.take(gathered, row_ids, axis=2)
        current = jnp.where(segment_ordinal == 0, start_state, arriving)
        onehot = (setting_ids[None, :] == pattern[:, None]).astype(jnp.float32)
        expanded = (current[:, :, :, None] * onehot[None, :, None, :]).reshape(
            2 * batch_size, local_rows * settings_count
        )
        prod_real = jnp.dot(expanded, weight_real, precision=lax.Precision.HIGHEST)
        prod_imag = jnp.dot(expanded, weight_imag, precision=lax.Precision.HIGHEST)
        out_real = prod_real[:batch_size] - prod_imag[batch_size:]
        out_imag = prod_imag[:batch_size] + prod_real[batch_size:]
        partial_value = jnp.stack([out_real, out_imag])
        term_real = jnp.dot(out_real, probe_re, precision=lax.Precision.HIGHEST) - jnp.dot(
            out_imag, probe_im, precision=lax.Precision.HIGHEST
        )
        term_imag = jnp.dot(out_real, probe_im, precision=lax.Precision.HIGHEST) + jnp.dot(
            out_imag, probe_re, precision=lax.Precision.HIGHEST
        )
        intersection_terms = jnp.stack([term_real, term_imag])[:, None, :]
        previous = lax.dynamic_slice_in_dim(buffer, clipped, 1, 1)
        updated = jnp.where(active, intersection_terms, previous)
        buffer = lax.dynamic_update_slice_in_dim(buffer, updated, clipped, 1)
        summed = lax.psum_scatter(partial_value, "stem", scatter_dimension=2, tiled=True)
        incoming = from_behind(summed, "section", 1)
        return (incoming, buffer)

    initial_incoming = jnp.zeros((2, batch_size, local_rows), jnp.float32)
    first_buffer = jnp.zeros((2, micro_count, batch_size), jnp.float32)
    time_steps = micro_count + section_count - 1
    final_incoming, buffer = lax.fori_loop(0, time_steps, advance, (initial_incoming, first_buffer))
    amplitudes = lax.psum(buffer, "stem")
    return amplitudes[None]


def solution(mesh):
    return jax.shard_map(
        local,
        mesh=mesh,
        in_specs=(
            P("section", None, None, None),
            P(),
            P("section", None, "stem", None, None),
            P("section", None, None),
            P(),
        ),
        out_specs=P("section", None, None, None),
        check_vma=False,
    )
```

profile of v0, /device:TPU:0, one launch (start us, length us, event | category | flops | bytes accessed | tf_op | source)
XLA Modules:
  0.0 622.9 jit_solution(6774410743164879172)
XLA Ops:
  9.3 21.2 %slice_bitcast_fusion = (f32[2048,2048]{1,0:T(8,128)}, f32[2048,2048]{1,0:T(8,128)}) fusion(f32[1,2,256,8,2048]{4,3,2,1,0:T(8,128)} %param.9), kind=kLoop, calls=%fused_computation.29 | loop fusion | bytes 67108864 | tf_op jit(solution)/shard_map/reshape;squeeze | solution.py:26
  30.6 571.3 %while.17 = (s32[]{:T(128)}, f32[2,32,256]{2,1,0:T(8,128)S(1)}, f32[2,4,32]{2,1,0:T(4,128)S(1)}, pred[]{:T(512)}, s32[256]{0:T(256)S(1)}, /*index=5*/s32[]{:T(12...) while((s32[]{:T(128)}, f32[2,32,256]{2,1,0:T(8,128)S(1)}, ...), condition=%wide.region_3.4_spmd.clone, body=%wide.region_1.3_spmd.clone.sunk | while | flops 6446288896 | bytes 113100216 | solution.py:71
  30.7 16.5 %all_gather.10 = f32[2,32,2048]{2,1,0:T(8,128)S(1)} all-gather(f32[2,32,256]{2,1,0:T(8,128)S(1)} %get-tuple-element.424), channel_id=1, replica_groups=mesh['section'=4,'stem'=8] {'stem'}, dimensions={2}, use_global_device_ids=true | all-gather | bytes 589824 | tf_op jit(solution)/shard_map/while/body/eval_jaxpr/all_gather | solution.py:42
  52.2 13.9 %fusion.48 = f32[64,2048]{1,0:T(8,128)S(1)} fusion(f32[64,2048]{0,1:T(8,128)S(1)} %mul.72, f32[2048,2048]{1,0:T(8,128)} %get-tuple-element.447), kind=kOutput, calls=%fused_computation.41.clone.1 | convolution fusion | flops 3221225472 | bytes 17825792 | tf_op jit(solution)/shard_map/while/body/eval_jaxpr/dot_general | solution.py:50
  78.6 31.1 %reduce-scatter.2.cloned.1.call-done = f32[2,32,256]{2,1,0:T(8,128)} async-done(((f32[2,32,2048]{2,1,0:T(8,128)}), f32[2,32,256]{2,1,0:T(8,128)}) %reduce-scatter.2.cloned.1.call-update) | async-done | bytes 65552 | tf_op jit(solution)/shard_map/while/body/eval_jaxpr/reduce_scatter | solution.py:64
  115.3 14.9 %all_gather.10 = f32[2,32,2048]{2,1,0:T(8,128)S(1)} all-gather(f32[2,32,256]{2,1,0:T(8,128)S(1)} %get-tuple-element.424), channel_id=1, replica_groups=mesh['section'=4,'stem'=8] {'stem'}, dimensions={2}, use_global_device_ids=true | all-gather | bytes 589824 | tf_op jit(solution)/shard_map/while/body/eval_jaxpr/all_gather | solution.py:42
  135.2 13.9 %fusion.48 = f32[64,2048]{1,0:T(8,128)S(1)} fusion(f32[64,2048]{0,1:T(8,128)S(1)} %mul.72, f32[2048,2048]{1,0:T(8,128)} %get-tuple-element.447), kind=kOutput, calls=%fused_computation.41.clone.1 | convolution fusion | flops 3221225472 | bytes 17825792 | tf_op jit(solution)/shard_map/while/body/eval_jaxpr/dot_general | solution.py:50
  161.6 29.2 %reduce-scatter.2.cloned.1.call-done = f32[2,32,256]{2,1,0:T(8,128)} async-done(((f32[2,32,2048]{2,1,0:T(8,128)}), f32[2,32,256]{2,1,0:T(8,128)}) %reduce-scatter.2.cloned.1.call-update) | async-done | bytes 65552 | tf_op jit(solution)/shard_map/while/body/eval_jaxpr/reduce_scatter | solution.py:64
  196.3 14.9 %all_gather.10 = f32[2,32,2048]{2,1,0:T(8,128)S(1)} all-gather(f32[2,32,256]{2,1,0:T(8,128)S(1)} %get-tuple-element.424), channel_id=1, replica_groups=mesh['section'=4,'stem'=8] {'stem'}, dimensions={2}, use_global_device_ids=true | all-gather | bytes 589824 | tf_op jit(solution)/shard_map/while/body/eval_jaxpr/all_gather | solution.py:42
  216.3 13.9 %fusion.48 = f32[64,2048]{1,0:T(8,128)S(1)} fusion(f32[64,2048]{0,1:T(8,128)S(1)} %mul.72, f32[2048,2048]{1,0:T(8,128)} %get-tuple-element.447), kind=kOutput, calls=%fused_computation.41.clone.1 | convolution fusion | flops 3221225472 | bytes 17825792 | tf_op jit(solution)/shard_map/while/body/eval_jaxpr/dot_general | solution.py:50
  242.7 29.3 %reduce-scatter.2.cloned.1.call-done = f32[2,32,256]{2,1,0:T(8,128)} async-done(((f32[2,32,2048]{2,1,0:T(8,128)}), f32[2,32,256]{2,1,0:T(8,128)}) %reduce-scatter.2.cloned.1.call-update) | async-done | bytes 65552 | tf_op jit(solution)/shard_map/while/body/eval_jaxpr/reduce_scatter | solution.py:64
  277.3 14.9 %all_gather.10 = f32[2,32,2048]{2,1,0:T(8,128)S(1)} all-gather(f32[2,32,256]{2,1,0:T(8,128)S(1)} %get-tuple-element.424), channel_id=1, replica_groups=mesh['section'=4,'stem'=8] {'stem'}, dimensions={2}, use_global_device_ids=true | all-gather | bytes 589824 | tf_op jit(solution)/shard_map/while/body/eval_jaxpr/all_gather | solution.py:42
  297.3 13.9 %fusion.48 = f32[64,2048]{1,0:T(8,128)S(1)} fusion(f32[64,2048]{0,1:T(8,128)S(1)} %mul.72, f32[2048,2048]{1,0:T(8,128)} %get-tuple-element.447), kind=kOutput, calls=%fused_computation.41.clone.1 | convolution fusion | flops 3221225472 | bytes 17825792 | tf_op jit(solution)/shard_map/while/body/eval_jaxpr/dot_general | solution.py:50
  323.7 29.5 %reduce-scatter.2.cloned.1.call-done = f32[2,32,256]{2,1,0:T(8,128)} async-done(((f32[2,32,2048]{2,1,0:T(8,128)}), f32[2,32,256]{2,1,0:T(8,128)}) %reduce-scatter.2.cloned.1.call-update) | async-done | bytes 65552 | tf_op jit(solution)/shard_map/while/body/eval_jaxpr/reduce_scatter | solution.py:64
  358.5 14.9 %all_gather.10 = f32[2,32,2048]{2,1,0:T(8,128)S(1)} all-gather(f32[2,32,256]{2,1,0:T(8,128)S(1)} %get-tuple-element.424), channel_id=1, replica_groups=mesh['section'=4,'stem'=8] {'stem'}, dimensions={2}, use_global_device_ids=true | all-gather | bytes 589824 | tf_op jit(solution)/shard_map/while/body/eval_jaxpr/all_gather | solution.py:42
  378.4 13.9 %fusion.48 = f32[64,2048]{1,0:T(8,128)S(1)} fusion(f32[64,2048]{0,1:T(8,128)S(1)} %mul.72, f32[2048,2048]{1,0:T(8,128)} %get-tuple-element.447), kind=kOutput, calls=%fused_computation.41.clone.1 | convolution fusion | flops 3221225472 | bytes 17825792 | tf_op jit(solution)/shard_map/while/body/eval_jaxpr/dot_general | solution.py:50
  404.8 29.1 %reduce-scatter.2.cloned.1.call-done = f32[2,32,256]{2,1,0:T(8,128)} async-done(((f32[2,32,2048]{2,1,0:T(8,128)}), f32[2,32,256]{2,1,0:T(8,128)}) %reduce-scatter.2.cloned.1.call-update) | async-done | bytes 65552 | tf_op jit(solution)/shard_map/while/body/eval_jaxpr/reduce_scatter | solution.py:64
  439.5 14.9 %all_gather.10 = f32[2,32,2048]{2,1,0:T(8,128)S(1)} all-gather(f32[2,32,256]{2,1,0:T(8,128)S(1)} %get-tuple-element.424), channel_id=1, replica_groups=mesh['section'=4,'stem'=8] {'stem'}, dimensions={2}, use_global_device_ids=true | all-gather | bytes 589824 | tf_op jit(solution)/shard_map/while/body/eval_jaxpr/all_gather | solution.py:42
  459.5 13.9 %fusion.48 = f32[64,2048]{1,0:T(8,128)S(1)} fusion(f32[64,2048]{0,1:T(8,128)S(1)} %mul.72, f32[2048,2048]{1,0:T(8,128)} %get-tuple-element.447), kind=kOutput, calls=%fused_computation.41.clone.1 | convolution fusion | flops 3221225472 | bytes 17825792 | tf_op jit(solution)/shard_map/while/body/eval_jaxpr/dot_general | solution.py:50
  485.9 29.1 %reduce-scatter.2.cloned.1.call-done = f32[2,32,256]{2,1,0:T(8,128)} async-done(((f32[2,32,2048]{2,1,0:T(8,128)}), f32[2,32,256]{2,1,0:T(8,128)}) %reduce-scatter.2.cloned.1.call-update) | async-done | bytes 65552 | tf_op jit(solution)/shard_map/while/body/eval_jaxpr/reduce_scatter | solution.py:64
  520.8 15.0 %all_gather.10 = f32[2,32,2048]{2,1,0:T(8,128)S(1)} all-gather(f32[2,32,256]{2,1,0:T(8,128)S(1)} %get-tuple-element.424), channel_id=1, replica_groups=mesh['section'=4,'stem'=8] {'stem'}, dimensions={2}, use_global_device_ids=true | all-gather | bytes 589824 | tf_op jit(solution)/shard_map/while/body/eval_jaxpr/all_gather | solution.py:42
  540.8 13.9 %fusion.48 = f32[64,2048]{1,0:T(8,128)S(1)} fusion(f32[64,2048]{0,1:T(8,128)S(1)} %mul.72, f32[2048,2048]{1,0:T(8,128)} %get-tuple-element.447), kind=kOutput, calls=%fused_computation.41.clone.1 | convolution fusion | flops 3221225472 | bytes 17825792 | tf_op jit(solution)/shard_map/while/body/eval_jaxpr/dot_general | solution.py:50
  567.2 28.9 %reduce-scatter.2.cloned.1.call-done = f32[2,32,256]{2,1,0:T(8,128)} async-done(((f32[2,32,2048]{2,1,0:T(8,128)}), f32[2,32,256]{2,1,0:T(8,128)}) %reduce-scatter.2.cloned.1.call-update) | async-done | bytes 65552 | tf_op jit(solution)/shard_map/while/body/eval_jaxpr/reduce_scatter | solution.py:64
  601.9 14.2 %psum.7 = f32[1,2,4,32]{3,2,1,0:T(4,128)} all-reduce(f32[1,2,4,32]{3,2,1,0:T(4,128)S(1)} %bitcast.124), channel_id=1, replica_groups=mesh['section'=4,'stem'=8] {'stem'}, use_global_device_ids=true, to_apply=%region_4.5 | all-reduce | flops 256 | bytes 2048 | tf_op jit(solution)/shard_map/psum | solution.py:72
  (197 shorter events, 163.1 us)
Async XLA Ops:
  9.3 21.2 %copy-start.1 = (f32[1,2,2048]{2,1,0:T(2,128)S(1)}, f32[1,2,2048]{2,1,0:T(2,128)}, u32[]{:S(2)}) copy-start(f32[1,2,2048]{2,1,0:T(2,128)} %param.10) | copy-start | bytes 49156
  9.3 21.2 %copy-start.2 = (s32[1,4,32,3]{2,1,3,0:T(4,128)S(1)}, s32[1,4,32,3]{2,1,3,0:T(4,128)}, u32[]{:S(2)}) copy-start(s32[1,4,32,3]{2,1,3,0:T(4,128)} %param.7) | copy-start | bytes 4612
  30.6 79.1 %reduce-scatter.2.cloned.1.call-start = ((), (), s32[]{:S(2)}) async-start(), calls=%async_computation.1 | async-start | bytes 589824 | tf_op jit(solution)/shard_map/while/body/eval_jaxpr/reduce_scatter | solution.py:64
  52.2 13.9 %copy-start = (f32[2048,2048]{1,0:T(8,128)S(1)}, f32[2048,2048]{1,0:T(8,128)}, u32[]{:S(2)}) copy-start(f32[2048,2048]{1,0:T(8,128)} %get-tuple-element.446) | copy-start | bytes 50331652 | tf_op jit(solution)/shard_map/while
  109.7 5.5 collective-permute-start
  115.2 75.6 %reduce-scatter.2.cloned.1.call-start = ((), (), s32[]{:S(2)}) async-start(), calls=%async_computation.1 | async-start | bytes 589824 | tf_op jit(solution)/shard_map/while/body/eval_jaxpr/reduce_scatter | solution.py:64
  135.2 13.9 %copy-start = (f32[2048,2048]{1,0:T(8,128)S(1)}, f32[2048,2048]{1,0:T(8,128)}, u32[]{:S(2)}) copy-start(f32[2048,2048]{1,0:T(8,128)} %get-tuple-element.446) | copy-start | bytes 50331652 | tf_op jit(solution)/shard_map/while
  190.8 5.4 collective-permute-start
  196.3 75.7 %reduce-scatter.2.cloned.1.call-start = ((), (), s32[]{:S(2)}) async-start(), calls=%async_computation.1 | async-start | bytes 589824 | tf_op jit(solution)/shard_map/while/body/eval_jaxpr/reduce_scatter | solution.py:64
  216.2 13.9 %copy-start = (f32[2048,2048]{1,0:T(8,128)S(1)}, f32[2048,2048]{1,0:T(8,128)}, u32[]{:S(2)}) copy-start(f32[2048,2048]{1,0:T(8,128)} %get-tuple-element.446) | copy-start | bytes 50331652 | tf_op jit(solution)/shard_map/while
  272.0 5.3 collective-permute-start
  277.3 75.9 %reduce-scatter.2.cloned.1.call-start = ((), (), s32[]{:S(2)}) async-start(), calls=%async_computation.1 | async-start | bytes 589824 | tf_op jit(solution)/shard_map/while/body/eval_jaxpr/reduce_scatter | solution.py:64
  297.2 13.9 %copy-start = (f32[2048,2048]{1,0:T(8,128)S(1)}, f32[2048,2048]{1,0:T(8,128)}, u32[]{:S(2)}) copy-start(f32[2048,2048]{1,0:T(8,128)} %get-tuple-element.446) | copy-start | bytes 50331652 | tf_op jit(solution)/shard_map/while
  353.1 5.3 collective-permute-start
  358.5 75.5 %reduce-scatter.2.cloned.1.call-start = ((), (), s32[]{:S(2)}) async-start(), calls=%async_computation.1 | async-start | bytes 589824 | tf_op jit(solution)/shard_map/while/body/eval_jaxpr/reduce_scatter | solution.py:64
  378.4 13.9 %copy-start = (f32[2048,2048]{1,0:T(8,128)S(1)}, f32[2048,2048]{1,0:T(8,128)}, u32[]{:S(2)}) copy-start(f32[2048,2048]{1,0:T(8,128)} %get-tuple-element.446) | copy-start | bytes 50331652 | tf_op jit(solution)/shard_map/while
  433.9 5.5 collective-permute-start
  439.5 75.5 %reduce-scatter.2.cloned.1.call-start = ((), (), s32[]{:S(2)}) async-start(), calls=%async_computation.1 | async-start | bytes 589824 | tf_op jit(solution)/shard_map/while/body/eval_jaxpr/reduce_scatter | solution.py:64
  459.4 13.9 %copy-start = (f32[2048,2048]{1,0:T(8,128)S(1)}, f32[2048,2048]{1,0:T(8,128)}, u32[]{:S(2)}) copy-start(f32[2048,2048]{1,0:T(8,128)} %get-tuple-element.446) | copy-start | bytes 50331652 | tf_op jit(solution)/shard_map/while
  515.0 5.8 collective-permute-start
  520.8 75.4 %reduce-scatter.2.cloned.1.call-start = ((), (), s32[]{:S(2)}) async-start(), calls=%async_computation.1 | async-start | bytes 589824 | tf_op jit(solution)/shard_map/while/body/eval_jaxpr/reduce_scatter | solution.py:64
  540.8 13.9 %copy-start = (f32[2048,2048]{1,0:T(8,128)S(1)}, f32[2048,2048]{1,0:T(8,128)}, u32[]{:S(2)}) copy-start(f32[2048,2048]{1,0:T(8,128)} %get-tuple-element.446) | copy-start | bytes 50331652 | tf_op jit(solution)/shard_map/while
  596.2 5.7 collective-permute-start
Sparse Core Ops, SparseCore 0:
  77.4 32.2 reduce-scatter.1
  160.4 30.3 reduce-scatter.1
  241.4 30.5 reduce-scatter.1
  322.4 30.6 reduce-scatter.1
  403.6 30.2 reduce-scatter.1
  484.6 30.3 reduce-scatter.1
  566.0 30.1 reduce-scatter.1
where the time goes:
time: 624 us; the launch traced here: 623 us
  waiting for transfers between devices  221 us (35%)
  matrix products  178 us (29%)
  blocking collectives  120 us (19%)
  local copies, waits for them, and re-layouts  45.5 us (7%)
  starting transfers between devices  23.2 us (4%)
  other arithmetic  20 us (3%)
  between operations  13.5 us (2%)
    reduce_scatter x7, waiting for transfers between devices, advance(): lax.psum_scatter(partial_value, 'stem', scatter_dimension=2, tiled=True)  206 us
    all_gather x7, blocking collectives, advance(): gathered = lax.all_gather(incoming, 'stem', axis=2, tiled=True)  106 us
    dot_general x7, matrix products, advance(): prod_imag = jnp.dot(expanded, weight_imag, precision=lax.Precision.HIGHEST)  97.4 us
    dot_general x7, matrix products, advance(): prod_real = jnp.dot(expanded, weight_real, precision=lax.Precision.HIGHEST)  71.4 us
    ppermute x7, starting transfers between devices, from_behind(): return lax.ppermute(block, axis, route)  23.1 us
    another operation x1, local copies, waits for them, and re-layouts, local(): weight_imag = stem_tensor[0, 1].reshape(local_rows * settings_count, width)  21.2 us
    ppermute x7, waiting for transfers between devices, from_behind(): return lax.ppermute(block, axis, route)  15 us
    psum x1, blocking collectives, local(): amplitudes = lax.psum(buffer, 'stem')  14.2 us
  transfers between devices with their start and end apart: 14, of which 14 were waited for; matrix products, arithmetic and copies ran while one was open for 2% of the time, Pallas kernels for 0%

commit v1 on v0

v1 whole, which is shorter than its diff:
```python
import jax
import jax.numpy as jnp
from jax import lax
from jax.sharding import PartitionSpec as P

HIGH = lax.Precision.HIGH
HIGHEST = lax.Precision.HIGHEST


def halves(x):
    hi = lax.reduce_precision(x, 8, 7)
    return hi.astype(jnp.bfloat16), (x - hi).astype(jnp.bfloat16)


def select_columns(x, chosen):
    rows = x.shape[0]
    pick = (jnp.arange(x.shape[1], dtype=jnp.int32)[:, None] == chosen[None, :]).astype(jnp.bfloat16)
    hi, lo = halves(x)
    both = jnp.dot(jnp.concatenate([hi, lo]), pick, preferred_element_type=jnp.float32)
    return both[:rows] + both[rows:]


def local(bitstrings, boundary, stem_tensor, probe_vectors, inbound_permutations):
    section = lax.axis_index("section")
    sections = lax.axis_size("section")
    rank = lax.axis_index("stem")
    rows, settings, width = stem_tensor.shape[2:]
    bonds = boundary.shape[1]
    micro, batch, qubits = bitstrings.shape[1:]
    count = micro * batch
    powers = jnp.left_shift(jnp.int32(1), jnp.arange(qubits, dtype=jnp.int32))
    own_setting = jnp.sum(bitstrings[0] * powers, axis=-1).reshape(count)
    setting = lax.all_gather(own_setting, "section")
    probe = probe_vectors[0]
    perm = inbound_permutations

    def flat(plane):
        return stem_tensor[0, plane].reshape(rows * settings, width)

    def own_rows(row):
        return lax.dynamic_slice_in_dim(row, rank * rows, rows)

    zeros_a = jnp.zeros((2 * settings, bonds), jnp.float32)

    def first_forward():
        t_re, t_im = stem_tensor[0, 0], stem_tensor[0, 1]
        b = jnp.dot(
            boundary,
            (jnp.arange(bonds, dtype=jnp.int32)[:, None] == own_rows(perm[0])[None, :]).astype(jnp.float32),
            precision=HIGHEST,
        )
        b_re, b_im = b[0][:, None, None], b[1][:, None, None]
        u_re = jnp.sum(b_re * t_re - b_im * t_im, axis=0)
        u_im = jnp.sum(b_re * t_im + b_im * t_re, axis=0)
        return jnp.concatenate([u_re, u_im])

    def last_backward():
        t_re, t_im = stem_tensor[0, 0], stem_tensor[0, 1]
        v_re = jnp.sum(t_re * probe[0] - t_im * probe[1], axis=-1)
        v_im = jnp.sum(t_re * probe[1] + t_im * probe[0], axis=-1)
        v = jnp.concatenate([v_re.T, v_im.T])
        return lax.dynamic_update_slice_in_dim(zeros_a, v, rank * rows, 1)

    idle = lambda: zeros_a
    vectors = lax.switch(section, [first_forward, idle, idle, last_backward])

    def product_with_probe(v_re, v_im):
        return (
            jnp.dot(v_re, probe[0], precision=HIGHEST) - jnp.dot(v_im, probe[1], precision=HIGHEST),
            jnp.dot(v_re, probe[1], precision=HIGHEST) + jnp.dot(v_im, probe[0], precision=HIGHEST),
        )

    amp_first = jnp.stack(product_with_probe(vectors[:settings], vectors[settings:]))
    moved = lax.ppermute(vectors, "section", [(0, 1), (3, 2)])
    vectors = lax.psum(moved, "stem")

    ends = settings + 1
    pairs = settings * settings
    zeros_u = jnp.zeros((2 * pairs, bonds), jnp.float32)
    zeros_w = jnp.zeros((rows, settings * 2 * ends), jnp.float32)
    zeros_p = jnp.zeros((2, pairs), jnp.float32)

    def second_forward():
        x = select_columns(vectors, own_rows(perm[1])).reshape(2, settings, 1, rows, 1)
        same = jnp.eye(settings, dtype=jnp.float32).reshape(1, 1, settings, 1, settings)
        spread = (x * same).reshape(2 * pairs, rows * settings)
        p_re = jnp.dot(spread, flat(0), precision=HIGH)
        p_im = jnp.dot(spread, flat(1), precision=HIGH)
        u_re = p_re[:pairs] - p_im[pairs:]
        u_im = p_im[:pairs] + p_re[pairs:]
        amp = jnp.stack(product_with_probe(u_re, u_im))
        u = select_columns(jnp.concatenate([u_re, u_im]), perm[2])
        return u, zeros_w, amp

    def second_backward():
        place = (perm[3][:, None] == jnp.arange(bonds, dtype=jnp.int32)[None, :]).astype(jnp.bfloat16)
        hi, lo = halves(vectors)
        both = jnp.dot(jnp.concatenate([hi, lo]), place, preferred_element_type=jnp.float32)
        v = (both[: 2 * settings] + both[2 * settings :]).reshape(2, settings, bonds)
        v = jnp.concatenate([v, probe[:, None, :]], axis=1).reshape(2 * ends, bonds)
        q_re = lax.dot_general(flat(0), v, (((1,), (1,)), ((), ())), precision=HIGH)
        q_im = lax.dot_general(flat(1), v, (((1,), (1,)), ((), ())), precision=HIGH)
        w_re = q_re[:, :ends] - q_im[:, ends:]
        w_im = q_re[:, ends:] + q_im[:, :ends]
        w = jnp.concatenate([w_re, w_im], axis=1).reshape(rows, settings * 2 * ends)
        return zeros_u, w, zeros_p

    none = lambda: (zeros_u, zeros_w, zeros_p)
    u, w, amp_second = lax.switch(section, [none, second_forward, second_backward, none])
    w = lax.ppermute(w, "section", [(2, 1)])
    w = lax.all_gather(w, "stem", axis=0, tiled=True)
    joined = jnp.dot(u, w, precision=HIGH).reshape(2, pairs, settings, 2, ends)
    j_re = (joined[0, :, :, 0] - joined[1, :, :, 1]).reshape(pairs, settings * ends)
    j_im = (joined[0, :, :, 1] + joined[1, :, :, 0]).reshape(pairs, settings * ends)

    onehot = lambda ids, size: (ids[:, None] == jnp.arange(size, dtype=jnp.int32)[None, :]).astype(jnp.float32)
    front = onehot(setting[0] * settings + setting[1], pairs)
    first = jnp.dot(amp_first, onehot(setting[0], settings).T, precision=HIGHEST)
    first = jnp.where(section == 0, first, 0.0)
    second = jnp.dot(amp_second, front.T, precision=HIGHEST)
    third_pick = onehot(setting[2] * ends + settings, settings * ends)
    fourth_pick = onehot(setting[2] * ends + setting[3], settings * ends)
    rows_re = jnp.dot(front, j_re, precision=HIGHEST)
    rows_im = jnp.dot(front, j_im, precision=HIGHEST)
    third = jnp.stack([jnp.sum(rows_re * third_pick, axis=1), jnp.sum(rows_im * third_pick, axis=1)])
    fourth = jnp.stack([jnp.sum(rows_re * fourth_pick, axis=1), jnp.sum(rows_im * fourth_pick, axis=1)])
    partial = jnp.stack([first, second, third, fourth])
    total = lax.psum(partial, ("section", "stem"))
    own = lax.dynamic_index_in_dim(total, section, 0, False)
    return own.reshape(1, 2, micro, batch)


def solution(mesh):
    return jax.shard_map(
        local,
        mesh=mesh,
        in_specs=(
            P("section", None, None, None),
            P(),
            P("section", None, "stem", None, None),
            P("section", None, None),
            P(),
        ),
        out_specs=P("section", None, None, None),
        check_vma=False,
    )
```

time: 624 us -> 224 us (0.36)
  matrix products: 178 us -> 7.6 us
  waiting for transfers between devices: 221 us -> 80.3 us
  local copies, waits for them, and re-layouts: 45.5 us -> 3.15 us
  starting transfers between devices: 23.2 us -> 2.01 us
  blocking collectives: 120 us -> 103 us
  other arithmetic: 20 us -> 13.1 us
    reduce_scatter x7 -> x0, waiting for transfers between devices: 206 us -> none  [advance(): lax.psum_scatter(partial_value, 'stem', scatter_dimension=2, tiled=True)]
    dot_general x42 -> x10, matrix products: 178 us -> 7.6 us  [the longest x1 3.4 us: local(): joined = jnp.dot(u, w, precision=HIGH).reshape(2, pairs, settings, 2, ends)]
    psum x0 -> x1, waiting for transfers between devices: none -> 58.5 us  [local(): vectors = lax.psum(moved, 'stem')]
    all_gather x7 -> x1, blocking collectives: 106 us -> 63 us  [local(): setting = lax.all_gather(own_setting, 'section')]
    psum x1, blocking collectives: 14.2 us -> 40.2 us  [local(): total = lax.psum(partial, ('section', 'stem'))]
    ppermute x7 -> x2, starting transfers between devices: 23.1 us -> 1.96 us  [the longest x1 1.28 us: local(): moved = lax.ppermute(vectors, 'section', [(0, 1), (3, 2)])]
    another operation x1 -> x0, local copies, waits for them, and re-layouts: 21.2 us -> none  [local(): weight_imag = stem_tensor[0, 1].reshape(local_rows * settings_count, width)]
    all_gather x0 -> x1, waiting for transfers between devices: none -> 17.8 us  [local(): w = lax.all_gather(w, 'stem', axis=0, tiled=True)]
  transfers between devices with their start and end apart: 14 -> 4, of which waited for: 14 -> 3; matrix products, arithmetic and copies ran while one was open for 2% -> 1% of each run, Pallas kernels for 0% -> 0%
where the time goes in v1:
time: 224 us; the launch traced here: 223 us
  blocking collectives  103 us (46%)
  waiting for transfers between devices  80.3 us (36%)
  between operations  13.5 us (6%)
  other arithmetic  13.1 us (6%)
  matrix products  7.6 us (3%)
  local copies, waits for them, and re-layouts  3.15 us (1%)
    all_gather x1, blocking collectives, local(): setting = lax.all_gather(own_setting, 'section')  63 us
    psum x1, waiting for transfers between devices, local(): vectors = lax.psum(moved, 'stem')  58.5 us
    psum x1, blocking collectives, local(): total = lax.psum(partial, ('section', 'stem'))  40.2 us
    all_gather x1, waiting for transfers between devices, local(): w = lax.all_gather(w, 'stem', axis=0, tiled=True)  17.8 us
    reduce_sum x1, other arithmetic, first_forward(): u_re = jnp.sum(b_re * t_re - b_im * t_im, axis=0)  12.2 us
  transfers between devices with their start and end apart: 4, of which 3 were waited for; matrix products, arithmetic and copies ran while one was open for 1% of the time, Pallas kernels for 0%

profile of v1, /device:TPU:0, one launch (start us, length us, event | category | flops | bytes accessed | tf_op | source)
XLA Modules:
  0.0 223.1 jit_solution(2156276009823240268)
XLA Ops:
  6.5 15.1 %conditional.2 = (f32[16,2048]{1,0:T(8,128)}, f32[8,2048]{1,0:T(8,128)S(1)}, f32[8,2048]{1,0:T(8,128)S(1)}) conditional(s32[]{:T(128)} %clamp.4, (s32[4,2048]{1,0:T(4,128)}, s32[]{:T(128)}, f32[2,2048]{1,0:T(2,128)}, f32[1,2,256,8,2048]{4,3,2,1,0:T(8,128)}) %tuple.41, () %tuple.42, () %tuple.43, ...), branch_computations={%region_0.3_spmd, %region_3.4_spmd, %region_4.0_spmd, %region_5.8_... | conditional | flops 46661636 | bytes 34078796 | solution.py:65
  6.5 0.8 slice.108
  7.3 1.4 fusion.5
  8.8 12.2 %fusion.1 = (f32[8,2048]{1,0:T(8,128)S(1)}, f32[8,2048]{1,0:T(8,128)S(1)}) fusion(f32[1,2,256,8,2048]{4,3,2,1,0:T(8,128)} %get-tuple-element.43, f32[256]{0:T(256)S(1)} %bitcast.210, f32[256]{0:T(256)S(1)} %bitcast.209), kind=kLoop, calls=%fused_computation.3 | loop fusion | flops 33521664 | bytes 33687552 | tf_op jit(solution)/shard_map/cond/branch_0_fun/reduce_sum | solution.py:53
  21.0 0.6 pad_maximum_fusion
  21.6 1.3 collective-permute-start
  22.9 4.0 %collective-permute-done = f32[16,2048]{1,0:T(8,128)S(1)} collective-permute-done((f32[16,2048]{1,0:T(8,128)}, f32[16,2048]{1,0:T(8,128)S(1)}, u32[]{:S(2)}, u32[]{:S(2)}) %collective-permute-start) | collective-permute-done | bytes 131104 | tf_op jit(solution)/shard_map/ppermute | solution.py:74
  26.9 0.6 copy-done.3
  27.6 58.5 %all-reduce.2.cloned.1.call-done = f32[16,2048]{1,0:T(8,128)} async-done(((f32[16,2048]{1,0:T(8,128)}), f32[16,2048]{1,0:T(8,128)}) %all-reduce.2.cloned.1.call-update) | async-done | bytes 131088 | tf_op jit(solution)/shard_map/psum | solution.py:75
  86.1 0.4 conditional.3
  86.5 0.7 collective-permute-start.1
  87.2 0.7 copy-done.2
  88.1 63.0 %all-gather = s32[4,1,128]{2,1,0:T(1,128)S(1)} all-gather(s32[1,1,128]{2,1,0:T(1,128)S(1)} %reshape.101), channel_id=1, replica_groups=mesh['section'=4,'stem'=8] {'section'}, dimensions={0}, use_global_device_ids=true | all-gather | bytes 2560 | tf_op jit(solution)/shard_map/all_gather | solution.py:33
  151.1 0.9 convolution_bitcast_fusion.7
  152.1 0.3 convolution_bitcast_fusion.5
  152.3 0.3 fusion.67
  152.6 0.3 fusion.69
  153.1 0.3 convolution_bitcast_fusion.4
  153.4 17.8 %all-gather.3.cloned.1.call-done = f32[2048,144]{1,0:T(8,128)} async-done(((f32[256,144]{1,0:T(8,128)}), f32[2048,144]{1,0:T(8,128)}) %all-gather.3.cloned.1.call-update) | async-done | bytes 1179664 | tf_op jit(solution)/shard_map/all_gather | solution.py:111
  171.1 3.4 %fusion.95 = f32[128,144]{0,1:T(8,128)S(1)} fusion(f32[128,2048]{1,0:T(8,128)S(1)} %get-tuple-element.66, f32[2048,144]{1,0:T(8,128)} %all-gather.3.cloned.1.call-done), kind=kOutput, calls=%fused_computation.158 | convolution fusion | flops 226492416 | bytes 2301952 | tf_op jit(solution)/shard_map/dot_general | solution.py:112
  174.7 0.3 fusion.71
  175.0 0.3 select_reduce_fusion.2
  175.4 40.2 %psum.15 = f32[4,2,128]{2,1,0:T(2,128)S(1)} all-reduce(f32[4,2,128]{2,1,0:T(2,128)S(1)} %pad_maximum_fusion.5), channel_id=1, replica_groups=mesh['section'=4,'stem'=8] {'section','stem'}, use_global_device_ids=true, to_apply=%region_18.19 | all-reduce | flops 1024 | bytes 8192 | tf_op jit(solution)/shard_map/psum | solution.py:128
  215.5 0.7 reshape.100
  (27 shorter events, 0.8 us)
Async XLA Ops:
  6.5 79.5 %all-reduce.2.cloned.1.call-start = ((), (), s32[]{:S(2)}) async-start(), calls=%async_computation | async-start | bytes 262144 | tf_op jit(solution)/shard_map/psum | solution.py:75
  21.6 5.3 %collective-permute-start = (f32[16,2048]{1,0:T(8,128)}, f32[16,2048]{1,0:T(8,128)S(1)}, u32[]{:S(2)}, u32[]{:S(2)}) collective-permute-start(f32[16,2048]{1,0:T(8,128)} %get-tuple-element.64), channel_id=1, source_target_pairs={{0,8},{24,16},{1,9},{25,17},{2,10},{26,18},{3,11},{27,19},{4,12},{... | collective-permute-start | bytes 393224 | tf_op jit(solution)/shard_map/ppermute | solution.py:74
  26.9 0.6 copy-start.3
  27.6 143.6 %all-gather.3.cloned.1.call-start = ((), (), s32[]{:S(2)}) async-start(), calls=%async_computation.1 | async-start | bytes 2359296 | tf_op jit(solution)/shard_map/all_gather | solution.py:111
  86.1 1.9 copy-start.4
  86.1 66.0 %copy-start = (f32[1,2,2048]{2,1,0:T(2,128)S(1)}, f32[1,2,2048]{2,1,0:T(2,128)}, u32[]{:S(2)}) copy-start(f32[1,2,2048]{2,1,0:T(2,128)} %param.16) | copy-start | bytes 49156
  86.5 0.7 collective-permute-start.1
  87.2 0.7 copy-start.2
Sparse Core Ops, SparseCore 0:
  27.7 58.3 all-reduce.1
  88.0 83.0 all-gather.2

commit v2 on v1

--- a/solution.py
+++ b/solution.py
@@ -1,6 +1,10 @@
+import functools
+
 import jax
 import jax.numpy as jnp
 from jax import lax
+from jax.experimental import pallas as pl
+from jax.experimental.pallas import tpu as pltpu
 from jax.sharding import PartitionSpec as P
 
 HIGH = lax.Precision.HIGH
@@ -18,6 +22,203 @@
     hi, lo = halves(x)
     both = jnp.dot(jnp.concatenate([hi, lo]), pick, preferred_element_type=jnp.float32)
     return both[:rows] + both[rows:]
+
+
+MESH = pl.DeviceIdType.MESH
+VMEM = pl.BlockSpec(memory_space=pltpu.VMEM)
+
+
+def send(src, dst, send_sem, recv_sem, target):
+    return pltpu.make_async_remote_copy(
+        src_ref=src, dst_ref=dst, send_sem=send_sem, recv_sem=recv_sem, device_id=target, device_id_type=MESH
+    )
+
+
+def greet(targets):
+    barrier = pltpu.get_barrier_semaphore()
+    for target in targets:
+        pl.semaphore_signal(barrier, inc=1, device_id=target, device_id_type=MESH)
+    pl.semaphore_wait(barrier, len(targets))
+
+
+def call(kernel, outs, scratch, collective_id, *args):
+    return pl.pallas_call(
+        kernel,
+        out_shape=[jax.ShapeDtypeStruct(shape, jnp.float32) for shape in outs],
+        in_specs=[VMEM] * len(args),
+        out_specs=[VMEM] * len(outs),
+        scratch_shapes=scratch,
+        compiler_params=pltpu.CompilerParams(collective_id=collective_id, has_side_effects=True),
+    )(*args)
+
+
+def exchange_kernel(S, R, v_ref, set_ref, out_ref, sets_ref, land, total, s1, r1, s2, r2, s3, r3):
+    me_s, me_r = lax.axis_index("section"), lax.axis_index("stem")
+    partner = me_s + 1 - 2 * (me_s % 2)
+    ranks = [(me_r + d) % R for d in range(R)]
+    others = [(me_s + d) % S for d in range(S)]
+    greet(
+        [(me_s, r) for r in ranks[1:]] + [(partner, r) for r in ranks] + [(s, me_r) for s in others[1:]]
+    )
+    first = [
+        send(v_ref.at[ranks[d]], land.at[d - 1], s1.at[d - 1], r1.at[d - 1], (me_s, ranks[d])) for d in range(1, R)
+    ]
+    third = [
+        send(set_ref, sets_ref.at[me_s], s3.at[d - 1], r3.at[d - 1], (others[d], me_r)) for d in range(1, S)
+    ]
+    for copy in first + third:
+        copy.start()
+    sets_ref[me_s] = set_ref[...]
+    value = v_ref[me_r]
+    for d in range(1, R):
+        first[d - 1].wait_recv()
+        value = value + land[d - 1]
+    total[...] = value
+    second = [send(total, out_ref.at[me_r], s2.at[d], r2.at[d], (partner, ranks[d])) for d in range(R)]
+    for copy in second:
+        copy.start()
+    for copy in first:
+        copy.wait_send()
+    for copy in second + third:
+        copy.wait()
+
+
+def exchange(S, R, v, sets):
+    return call(
+        functools.partial(exchange_kernel, S, R),
+        [v.shape, (S,) + sets.shape],
+        [
+            pltpu.VMEM((R - 1,) + v.shape[1:], jnp.float32),
+            pltpu.VMEM(v.shape[1:], jnp.float32),
+            pltpu.SemaphoreType.DMA((R - 1,)),
+            pltpu.SemaphoreType.DMA((R - 1,)),
+            pltpu.SemaphoreType.DMA((R,)),
+            pltpu.SemaphoreType.DMA((R,)),
+            pltpu.SemaphoreType.DMA((S - 1,)),
+            pltpu.SemaphoreType.DMA((S - 1,)),
+        ],
+        1,
+        v,
+        sets,
+    )
+
+
+def meet_kernel(S, R, u_ref, w_ref, sum_ref, out_ref, land, su, ru, sw, rw):
+    me_s, me_r = lax.axis_index("section"), lax.axis_index("stem")
+    ranks = [(me_r + d) % R for d in range(R)]
+    greet([((me_s + e) % S, ranks[d]) for e in range(S) for d in range(R) if e + d])
+    far = [s for s in range(S) if s != 1]
+
+    def u_copies():
+        return [
+            send(u_ref.at[ranks[d] * S + s], land.at[me_r], su.at[d * S + s], ru.at[me_r], (s, ranks[d]))
+            for d in range(R)
+            for s in range(S)
+            if s != 1 or d
+        ]
+
+    def w_copies():
+        return [send(w_ref.at[s], out_ref, sw.at[s], rw.at[0], (s, me_r)) for s in range(S) if s != 2]
+
+    def arrived(rank):
+        send(land.at[rank], land.at[rank], su.at[0], ru.at[rank], (me_s, ranks[1])).wait_recv()
+
+    @pl.when(me_s == 1)
+    def _():
+        for copy in u_copies():
+            copy.start()
+        land[me_r] = u_ref[me_r * S + 1]
+
+    @pl.when(me_s == 2)
+    def _():
+        for copy in w_copies():
+            copy.start()
+        out_ref[...] = w_ref[2]
+
+    @pl.when(me_s == 1)
+    def _():
+        for d in range(1, R):
+            arrived(ranks[d])
+        for copy in u_copies():
+            copy.wait_send()
+
+    @pl.when(me_s != 1)
+    def _():
+        for rank in range(R):
+            arrived(rank)
+
+    @pl.when(me_s == 2)
+    def _():
+        for copy in w_copies():
+            copy.wait_send()
+
+    @pl.when(me_s != 2)
+    def _():
+        send(out_ref, out_ref, sw.at[0], rw.at[0], (me_s, ranks[1])).wait_recv()
+
+    value = land[0]
+    for rank in range(1, R):
+        value = value + land[rank]
+    sum_ref[...] = value
+
+
+def meet(S, R, u, w):
+    return call(
+        functools.partial(meet_kernel, S, R),
+        [u.shape[1:], w.shape[1:]],
+        [
+            pltpu.VMEM((R,) + u.shape[1:], jnp.float32),
+            pltpu.SemaphoreType.DMA((S * R,)),
+            pltpu.SemaphoreType.DMA((R,)),
+            pltpu.SemaphoreType.DMA((S,)),
+            pltpu.SemaphoreType.DMA((1,)),
+        ],
+        2,
+        u,
+        w,
+    )
+
+
+def total_kernel(S, R, p_ref, out_ref, land, half, far, s1, r1, s2, r2):
+    me_s, me_r = lax.axis_index("section"), lax.axis_index("stem")
+    near = [(me_s, (me_r + d) % R) for d in range(1, R)]
+    across = [((me_s + d) % S, me_r) for d in range(1, S)]
+    greet(near + across)
+    first = [send(p_ref, land.at[d], s1.at[d], r1.at[d], near[d]) for d in range(R - 1)]
+    for copy in first:
+        copy.start()
+    value = p_ref[...]
+    for d in range(R - 1):
+        first[d].wait_recv()
+        value = value + land[d]
+    half[...] = value
+    second = [send(half, far.at[d], s2.at[d], r2.at[d], across[d]) for d in range(S - 1)]
+    for copy in second:
+        copy.start()
+    for d in range(S - 1):
+        second[d].wait_recv()
+        value = value + far[d]
+    out_ref[...] = value
+    for copy in first + second:
+        copy.wait_send()
+
+
+def total(S, R, p):
+    return call(
+        functools.partial(total_kernel, S, R),
+        [p.shape],
+        [
+            pltpu.VMEM((R - 1,) + p.shape, jnp.float32),
+            pltpu.VMEM(p.shape, jnp.float32),
+            pltpu.VMEM((S - 1,) + p.shape, jnp.float32),
+            pltpu.SemaphoreType.DMA((R - 1,)),
+            pltpu.SemaphoreType.DMA((R - 1,)),
+            pltpu.SemaphoreType.DMA((S - 1,)),
+            pltpu.SemaphoreType.DMA((S - 1,)),
+        ],
+        3,
+        p,
+    )[0]
 
 
 def local(bitstrings, boundary, stem_tensor, probe_vectors, inbound_permutations):
@@ -30,7 +231,7 @@
     count = micro * batch
     powers = jnp.left_shift(jnp.int32(1), jnp.arange(qubits, dtype=jnp.int32))
     own_setting = jnp.sum(bitstrings[0] * powers, axis=-1).reshape(count)
-    setting = lax.all_gather(own_setting, "section")
+    ranks = lax.axis_size("stem")
     probe = probe_vectors[0]
     perm = inbound_permutations
 
@@ -71,26 +272,34 @@
         )
 
     amp_first = jnp.stack(product_with_probe(vectors[:settings], vectors[settings:]))
-    moved = lax.ppermute(vectors, "section", [(0, 1), (3, 2)])
-    vectors = lax.psum(moved, "stem")
+    blocks = vectors.reshape(2 * settings, ranks, rows).transpose(1, 0, 2)
+    own_block = jnp.broadcast_to(own_setting.astype(jnp.float32), (8, count))
+    blocks, setting = exchange(sections, ranks, blocks, own_block)
+    setting = setting[:, 0].astype(jnp.int32)
+    vectors = blocks.transpose(1, 0, 2).reshape(2 * settings, bonds)
 
     ends = settings + 1
     pairs = settings * settings
-    zeros_u = jnp.zeros((2 * pairs, bonds), jnp.float32)
-    zeros_w = jnp.zeros((rows, settings * 2 * ends), jnp.float32)
+    zeros_u = jnp.zeros((bonds, 2 * pairs), jnp.float32)
+    zeros_w = jnp.zeros((rows, 4 * pairs), jnp.float32)
     zeros_p = jnp.zeros((2, pairs), jnp.float32)
 
     def second_forward():
-        x = select_columns(vectors, own_rows(perm[1])).reshape(2, settings, 1, rows, 1)
-        same = jnp.eye(settings, dtype=jnp.float32).reshape(1, 1, settings, 1, settings)
-        spread = (x * same).reshape(2 * pairs, rows * settings)
+        x = select_columns(vectors, jnp.repeat(own_rows(perm[1]), settings))
+        same = jnp.arange(rows * settings, dtype=jnp.int32)[None, :] % settings
+        same = (same == jnp.arange(settings, dtype=jnp.int32)[:, None]).astype(jnp.float32)
+        spread = (x[:, None, :] * same[None]).reshape(2 * pairs, rows * settings)
         p_re = jnp.dot(spread, flat(0), precision=HIGH)
         p_im = jnp.dot(spread, flat(1), precision=HIGH)
         u_re = p_re[:pairs] - p_im[pairs:]
         u_im = p_im[:pairs] + p_re[pairs:]
         amp = jnp.stack(product_with_probe(u_re, u_im))
-        u = select_columns(jnp.concatenate([u_re, u_im]), perm[2])
-        return u, zeros_w, amp
+        hi, lo = halves(jnp.concatenate([u_re, u_im]))
+        pick = (perm[2][:, None] == jnp.arange(bonds, dtype=jnp.int32)[None, :]).astype(jnp.bfloat16)
+        both = lax.dot_general(
+            pick, jnp.concatenate([hi, lo]), (((1,), (1,)), ((), ())), preferred_element_type=jnp.float32
+        )
+        return both[:, : 2 * pairs] + both[:, 2 * pairs :], zeros_w, amp
 
     def second_backward():
         place = (perm[3][:, None] == jnp.arange(bonds, dtype=jnp.int32)[None, :]).astype(jnp.bfloat16)
@@ -102,31 +311,49 @@
         q_im = lax.dot_general(flat(1), v, (((1,), (1,)), ((), ())), precision=HIGH)
         w_re = q_re[:, :ends] - q_im[:, ends:]
         w_im = q_re[:, ends:] + q_im[:, :ends]
-        w = jnp.concatenate([w_re, w_im], axis=1).reshape(rows, settings * 2 * ends)
+        w_re, w_im = w_re.reshape(rows, settings, ends), w_im.reshape(rows, settings, ends)
+        w = jnp.concatenate(
+            [
+                w_re[:, :, :settings].reshape(rows, pairs),
+                w_im[:, :, :settings].reshape(rows, pairs),
+                w_re[:, :, settings],
+                w_im[:, :, settings],
+                jnp.zeros((rows, 2 * pairs - 2 * settings), jnp.float32),
+            ],
+            axis=1,
+        )
         return zeros_u, w, zeros_p
 
     none = lambda: (zeros_u, zeros_w, zeros_p)
     u, w, amp_second = lax.switch(section, [none, second_forward, second_backward, none])
-    w = lax.ppermute(w, "section", [(2, 1)])
-    w = lax.all_gather(w, "stem", axis=0, tiled=True)
-    joined = jnp.dot(u, w, precision=HIGH).reshape(2, pairs, settings, 2, ends)
-    j_re = (joined[0, :, :, 0] - joined[1, :, :, 1]).reshape(pairs, settings * ends)
-    j_im = (joined[0, :, :, 1] + joined[1, :, :, 0]).reshape(pairs, settings * ends)
+    share = rows // sections
+    u, w = meet(
+        sections, ranks, u.reshape(sections * ranks, share, 2 * pairs), w.reshape(sections, share, 4 * pairs)
+    )
+    joined = lax.dot_general(u, w, (((0,), (0,)), ((), ())), precision=HIGHEST)
+    upper, lower = joined[:pairs], joined[pairs:]
+    far_re = upper[:, :pairs] - lower[:, pairs : 2 * pairs]
+    far_im = upper[:, pairs : 2 * pairs] + lower[:, :pairs]
+    near = joined[:, 2 * pairs :]
+    near_re = near[:pairs, :settings] - near[pairs:, settings : 2 * settings]
+    near_im = near[:pairs, settings : 2 * settings] + near[pairs:, :settings]
 
     onehot = lambda ids, size: (ids[:, None] == jnp.arange(size, dtype=jnp.int32)[None, :]).astype(jnp.float32)
     front = onehot(setting[0] * settings + setting[1], pairs)
     first = jnp.dot(amp_first, onehot(setting[0], settings).T, precision=HIGHEST)
     first = jnp.where(section == 0, first, 0.0)
     second = jnp.dot(amp_second, front.T, precision=HIGHEST)
-    third_pick = onehot(setting[2] * ends + settings, settings * ends)
-    fourth_pick = onehot(setting[2] * ends + setting[3], settings * ends)
-    rows_re = jnp.dot(front, j_re, precision=HIGHEST)
-    rows_im = jnp.dot(front, j_im, precision=HIGHEST)
-    third = jnp.stack([jnp.sum(rows_re * third_pick, axis=1), jnp.sum(rows_im * third_pick, axis=1)])
-    fourth = jnp.stack([jnp.sum(rows_re * fourth_pick, axis=1), jnp.sum(rows_im * fourth_pick, axis=1)])
-    partial = jnp.stack([first, second, third, fourth])
-    total = lax.psum(partial, ("section", "stem"))
-    own = lax.dynamic_index_in_dim(total, section, 0, False)
+    third_pick = onehot(setting[2], settings)
+    fourth_pick = onehot(setting[2] * settings + setting[3], pairs)
+
+    def chosen(table, pick):
+        return jnp.sum(jnp.dot(front, table, precision=HIGHEST) * pick, axis=1)
+
+    third = jnp.stack([chosen(near_re, third_pick), chosen(near_im, third_pick)])
+    fourth = jnp.stack([chosen(far_re, fourth_pick), chosen(far_im, fourth_pick)])
+    partial = jnp.stack([first, second, third, fourth]).reshape(2 * sections, count)
+    summed = total(sections, ranks, partial).reshape(sections, 2, count)
+    own = lax.dynamic_index_in_dim(summed, section, 0, False)
     return own.reshape(1, 2, micro, batch)
 
 

time: 224 us -> 111 us (0.50)
  blocking collectives: 103 us -> 0 us
  Pallas kernels: 0 us -> 81.3 us
  waiting for transfers between devices: 80.3 us -> 0 us
  between operations: 13.5 us -> 0.08 us
  local copies, waits for them, and re-layouts: 3.15 us -> 5.55 us
    pallas_call x0 -> x3, Pallas kernels: none -> 81.3 us  [call(): pl.pallas_call(kernel, out_shape=[jax.ShapeDtypeStruct(shape, jnp.float32...]
    all_gather x1 -> x0, blocking collectives: 63 us -> none  [local(): setting = lax.all_gather(own_setting, 'section')]
    psum x1 -> x0, waiting for transfers between devices: 58.5 us -> none  [local(): vectors = lax.psum(moved, 'stem')]
    psum x1 -> x0, blocking collectives: 40.2 us -> none  [local(): total = lax.psum(partial, ('section', 'stem'))]
    all_gather x1 -> x0, waiting for transfers between devices: 17.8 us -> none  [local(): w = lax.all_gather(w, 'stem', axis=0, tiled=True)]
    ppermute x2 -> x0, waiting for transfers between devices: 3.99 us -> none  [the longest x1 3.98 us: local(): moved = lax.ppermute(vectors, 'section', [(0, 1), (3, 2)])]
    reshape x1 -> x4, local copies, waits for them, and re-layouts: 0.14 us -> 2.71 us  [the longest x1 1.61 us: local(): blocks = vectors.reshape(2 * settings, ranks, rows).transpose(1, 0, 2)]
  transfers between devices with their start and end apart: 4 -> 0, of which waited for: 3 -> 0; matrix products, arithmetic and copies ran while one was open for 1% -> 0% of each run, Pallas kernels for 0% -> 0%
where the time goes in v2:
time: 111 us
  Pallas kernels  81.3 us (73%)
  other arithmetic  15 us (14%)
  matrix products  8.57 us (8%)
  local copies, waits for them, and re-layouts  5.55 us (5%)
    pallas_call x3, Pallas kernels, call(): pl.pallas_call(kernel, out_shape=[jax.ShapeDtypeStruct(shape, jnp.float32...  81.3 us
    reduce_sum x1, other arithmetic, first_forward(): u_re = jnp.sum(b_re * t_re - b_im * t_im, axis=0)  12.2 us

profile of v2, /device:TPU:0, one launch (start us, length us, event | category | flops | bytes accessed | tf_op | source)
XLA Modules:
  0.0 110.8 jit_solution(18440493432374746849)
XLA Ops:
  0.0 0.8 fusion.102
  0.9 0.6 broadcast_in_dim.35.set_ref
  1.5 15.1 %conditional.2 = (f32[16,2048]{1,0:T(8,128)}) conditional(s32[]{:T(128)} %clamp.4, (s32[4,2048]{1,0:T(4,128)}, s32[]{:T(128)}, f32[2,2048]{1,0:T(2,128)}, f32[1,2,256,8,2048]{4,3,2,1,0:T(8,128)}) %tuple.41, () %tuple.42, () %tuple.43, (f32[1,2,256,8,2048]{4,3,2,1,0:T(8,128)}, f32[2,2048]{1,0:T(2,128)}, ...), branch_computations={%region_0.3_spmd, %region_3.4_spmd, %region_4.0_spmd, %region_5.8_... | conditional | flops 46661636 | bytes 33991736 | solution.py:266
  1.5 0.8 slice.131
  2.3 1.4 %fusion.5 = f32[2,256]{1,0:T(2,128)S(1)} fusion(f32[2,2048]{1,0:T(2,128)} %get-tuple-element.75, s32[256]{0:T(256)S(1)} %bitcast.235), kind=kOutput, calls=%fused_computation.10 | convolution fusion | flops 13107200 | bytes 19456 | tf_op jit(solution)/shard_map/cond/branch_0_fun/dot_general | solution.py:248
  3.7 12.2 %fusion.1 = (f32[8,2048]{1,0:T(8,128)S(1)}, f32[8,2048]{1,0:T(8,128)S(1)}) fusion(f32[1,2,256,8,2048]{4,3,2,1,0:T(8,128)} %get-tuple-element.47, f32[256]{0:T(256)S(1)} %bitcast.234, f32[256]{0:T(256)S(1)} %bitcast.233), kind=kLoop, calls=%fused_computation.3 | loop fusion | flops 33521664 | bytes 33687552 | tf_op jit(solution)/shard_map/cond/branch_0_fun/reduce_sum | solution.py:254
  15.9 0.7 pad_maximum_fusion
  16.6 1.0 convolution_bitcast_fusion.5
  17.6 1.1 %fusion.83 = f32[1,8]{1,0:T(1,128)S(1)} fusion(f32[8]{0:T(128)S(1)} %convolution_bitcast_fusion.5, f32[16,2048]{1,0:T(8,128)} %get-tuple-element.130, f32[1,2,2048]{2,1,0:T(2,128)S(1)} %copy-done), kind=kOutput, calls=%fused_computation.129 | convolution fusion | flops 196616 | bytes 74272 | tf_op jit(solution)/shard_map/dot_general | solution.py:271
  18.8 1.1 convolution_bitcast_fusion.7
  19.8 1.1 fusion.81
  20.9 1.6 %copy.39 = f32[2,8,8,256]{3,2,0,1:T(8,128)} copy(f32[2,8,8,256]{3,2,1,0:T(8,128)} %bitcast.75) | data formatting | bytes 262144 | tf_op jit(solution)/shard_map/reshape | solution.py:275
  22.5 16.5 %shard_map.56 = (f32[8,16,256]{2,1,0:T(8,128)}, f32[4,8,128]{2,1,0:T(8,128)}) custom-call(f32[8,16,256]{2,1,0:T(8,128)} %bitcast.223, f32[8,128]{1,0:T(8,128)} %broadcast_in_dim.35.set_ref), custom_call_target="tpu_custom_call" | custom-call | tf_op jit(solution)/shard_map/pallas_call | solution.py:45
  39.1 0.7 slice_convert_fusion
  39.8 0.9 copy.35
  40.9 0.4 conditional.3
  41.6 46.1 %shard_map.57 = (f32[64,128]{1,0:T(8,128)}, f32[64,256]{1,0:T(8,128)}) custom-call(f32[32,64,128]{2,1,0:T(8,128)S(1)} %get-tuple-element.70.u_ref, f32[4,64,256]{2,1,0:T(8,128)S(1)} %get-tuple-element.71.w_ref), custom_call_target="tpu_custom_call" | custom-call | tf_op jit(solution)/shard_map/pallas_call | solution.py:45
  87.7 1.2 %fusion.116 = f32[128,256]{1,0:T(8,128)S(1)} fusion(f32[64,128]{1,0:T(8,128)} %get-tuple-element.72, f32[64,256]{1,0:T(8,128)} %get-tuple-element.73), kind=kOutput, calls=%fused_computation.182 | convolution fusion | flops 25165824 | bytes 229376 | tf_op jit(solution)/shard_map/dot_general | solution.py:333
  89.4 0.4 fusion.75
  89.8 0.3 fusion.76
  90.1 0.6 pad_maximum_fusion.4
  90.7 18.7 %shard_map.58 = f32[8,128]{1,0:T(8,128)} custom-call(f32[8,128]{1,0:T(8,128)} %bitcast.228), custom_call_target="tpu_custom_call" | custom-call | tf_op jit(solution)/shard_map/pallas_call | solution.py:45
  109.4 0.7 constant_dynamic-slice_fusion.2
  110.1 0.7 reshape.165
  (17 shorter events, 1.3 us)
Async XLA Ops:
  1.5 16.2 %copy-start = (f32[1,2,2048]{2,1,0:T(2,128)S(1)}, f32[1,2,2048]{2,1,0:T(2,128)}, u32[]{:S(2)}) copy-start(f32[1,2,2048]{2,1,0:T(2,128)} %param.16) | copy-start | bytes 49156

commit v3 on v2

--- a/solution.py
+++ b/solution.py
@@ -103,12 +103,13 @@
     )
 
 
-def meet_kernel(S, R, u_ref, w_ref, sum_ref, out_ref, land, su, ru, sw, rw):
+def meet_kernel(
+    S, R, u_ref, w_ref, f_ref, g_ref, h_ref, e_ref, sum_ref, land, out_ref, su, ru, sw, rw,
+    part, land1, half, far, s1, r1, s2, r2,
+):
     me_s, me_r = lax.axis_index("section"), lax.axis_index("stem")
     ranks = [(me_r + d) % R for d in range(R)]
     greet([((me_s + e) % S, ranks[d]) for e in range(S) for d in range(R) if e + d])
-    far = [s for s in range(S) if s != 1]
-
     def u_copies():
         return [
             send(u_ref.at[ranks[d] * S + s], land.at[me_r], su.at[d * S + s], ru.at[me_r], (s, ranks[d]))
@@ -159,38 +160,30 @@
     value = land[0]
     for rank in range(1, R):
         value = value + land[rank]
-    sum_ref[...] = value
-
-
-def meet(S, R, u, w):
-    return call(
-        functools.partial(meet_kernel, S, R),
-        [u.shape[1:], w.shape[1:]],
-        [
-            pltpu.VMEM((R,) + u.shape[1:], jnp.float32),
-            pltpu.SemaphoreType.DMA((S * R,)),
-            pltpu.SemaphoreType.DMA((R,)),
-            pltpu.SemaphoreType.DMA((S,)),
-            pltpu.SemaphoreType.DMA((1,)),
-        ],
-        2,
-        u,
-        w,
-    )
-
-
-def total_kernel(S, R, p_ref, out_ref, land, half, far, s1, r1, s2, r2):
-    me_s, me_r = lax.axis_index("section"), lax.axis_index("stem")
-    near = [(me_s, (me_r + d) % R) for d in range(1, R)]
+
+    def dot(a, b):
+        return jnp.dot(a, b, precision=HIGHEST, preferred_element_type=jnp.float32)
+
+    def put(row, a, b):
+        n = a.shape[1] // 2
+        part[row : row + 1, :] = jnp.sum(a[:, :n] * b[:, :n] - a[:, n:] * b[:, n:], axis=0, keepdims=True)
+        part[row + 1 : row + 2, :] = jnp.sum(a[:, :n] * b[:, n:] + a[:, n:] * b[:, :n], axis=0, keepdims=True)
+
+    front = dot(value, f_ref[...])
+    wide = out_ref.shape[1] // 2
+    part[0:4, :] = e_ref[0:4, :]
+    put(4, front, dot(out_ref[:, wide:], h_ref[...]))
+    put(6, front, dot(out_ref[:, :wide], g_ref[...]))
+
+    near = [(me_s, ranks[d]) for d in range(1, R)]
     across = [((me_s + d) % S, me_r) for d in range(1, S)]
-    greet(near + across)
-    first = [send(p_ref, land.at[d], s1.at[d], r1.at[d], near[d]) for d in range(R - 1)]
+    first = [send(part, land1.at[d], s1.at[d], r1.at[d], near[d]) for d in range(R - 1)]
     for copy in first:
         copy.start()
-    value = p_ref[...]
+    value = part[...]
     for d in range(R - 1):
         first[d].wait_recv()
-        value = value + land[d]
+        value = value + land1[d]
     half[...] = value
     second = [send(half, far.at[d], s2.at[d], r2.at[d], across[d]) for d in range(S - 1)]
     for copy in second:
@@ -198,26 +191,38 @@
     for d in range(S - 1):
         second[d].wait_recv()
         value = value + far[d]
-    out_ref[...] = value
+    sum_ref[...] = value
     for copy in first + second:
         copy.wait_send()
 
 
-def total(S, R, p):
+def meet(S, R, u, w, f, g, h, e):
     return call(
-        functools.partial(total_kernel, S, R),
-        [p.shape],
+        functools.partial(meet_kernel, S, R),
+        [e.shape],
         [
-            pltpu.VMEM((R - 1,) + p.shape, jnp.float32),
-            pltpu.VMEM(p.shape, jnp.float32),
-            pltpu.VMEM((S - 1,) + p.shape, jnp.float32),
+            pltpu.VMEM((R,) + u.shape[1:], jnp.float32),
+            pltpu.VMEM(w.shape[1:], jnp.float32),
+            pltpu.SemaphoreType.DMA((S * R,)),
+            pltpu.SemaphoreType.DMA((R,)),
+            pltpu.SemaphoreType.DMA((S,)),
+            pltpu.SemaphoreType.DMA((1,)),
+            pltpu.VMEM(e.shape, jnp.float32),
+            pltpu.VMEM((R - 1,) + e.shape, jnp.float32),
+            pltpu.VMEM(e.shape, jnp.float32),
+            pltpu.VMEM((S - 1,) + e.shape, jnp.float32),
             pltpu.SemaphoreType.DMA((R - 1,)),
             pltpu.SemaphoreType.DMA((R - 1,)),
             pltpu.SemaphoreType.DMA((S - 1,)),
             pltpu.SemaphoreType.DMA((S - 1,)),
         ],
-        3,
-        p,
+        2,
+        u,
+        w,
+        f,
+        g,
+        h,
+        e,
     )[0]
 
 
@@ -265,13 +270,7 @@
     idle = lambda: zeros_a
     vectors = lax.switch(section, [first_forward, idle, idle, last_backward])
 
-    def product_with_probe(v_re, v_im):
-        return (
-            jnp.dot(v_re, probe[0], precision=HIGHEST) - jnp.dot(v_im, probe[1], precision=HIGHEST),
-            jnp.dot(v_re, probe[1], precision=HIGHEST) + jnp.dot(v_im, probe[0], precision=HIGHEST),
-        )
-
-    amp_first = jnp.stack(product_with_probe(vectors[:settings], vectors[settings:]))
+    own_vectors = vectors
     blocks = vectors.reshape(2 * settings, ranks, rows).transpose(1, 0, 2)
     own_block = jnp.broadcast_to(own_setting.astype(jnp.float32), (8, count))
     blocks, setting = exchange(sections, ranks, blocks, own_block)
@@ -282,7 +281,24 @@
     pairs = settings * settings
     zeros_u = jnp.zeros((bonds, 2 * pairs), jnp.float32)
     zeros_w = jnp.zeros((rows, 4 * pairs), jnp.float32)
-    zeros_p = jnp.zeros((2, pairs), jnp.float32)
+    zeros_p = jnp.zeros((2, count), jnp.float32)
+
+    def onehot(ids, size):
+        return (jnp.arange(size, dtype=jnp.int32)[:, None] == ids[None, :]).astype(jnp.float32)
+
+    def twice(pick):
+        return jnp.kron(jnp.eye(2, dtype=jnp.float32), pick)
+
+    front = onehot(setting[0] * settings + setting[1], pairs)
+
+    def with_probe(v, pick):
+        m = lax.dot_general(v, probe, (((1,), (1,)), ((), ())), precision=HIGHEST)
+        n = m.shape[0] // 2
+        amp = jnp.stack([m[:n, 0] - m[n:, 1], m[:n, 1] + m[n:, 0]])
+        return jnp.dot(amp, pick, precision=HIGHEST)
+
+    def first_amplitudes():
+        return zeros_u, zeros_w, with_probe(own_vectors, onehot(setting[0], settings))
 
     def second_forward():
         x = select_columns(vectors, jnp.repeat(own_rows(perm[1]), settings))
@@ -293,8 +309,9 @@
         p_im = jnp.dot(spread, flat(1), precision=HIGH)
         u_re = p_re[:pairs] - p_im[pairs:]
         u_im = p_im[:pairs] + p_re[pairs:]
-        amp = jnp.stack(product_with_probe(u_re, u_im))
-        hi, lo = halves(jnp.concatenate([u_re, u_im]))
+        u = jnp.concatenate([u_re, u_im])
+        amp = with_probe(u, front)
+        hi, lo = halves(u)
         pick = (perm[2][:, None] == jnp.arange(bonds, dtype=jnp.int32)[None, :]).astype(jnp.bfloat16)
         both = lax.dot_general(
             pick, jnp.concatenate([hi, lo]), (((1,), (1,)), ((), ())), preferred_element_type=jnp.float32
@@ -325,34 +342,22 @@
         return zeros_u, w, zeros_p
 
     none = lambda: (zeros_u, zeros_w, zeros_p)
-    u, w, amp_second = lax.switch(section, [none, second_forward, second_backward, none])
+    u, w, amp = lax.switch(section, [first_amplitudes, second_forward, second_backward, none])
     share = rows // sections
-    u, w = meet(
-        sections, ranks, u.reshape(sections * ranks, share, 2 * pairs), w.reshape(sections, share, 4 * pairs)
-    )
-    joined = lax.dot_general(u, w, (((0,), (0,)), ((), ())), precision=HIGHEST)
-    upper, lower = joined[:pairs], joined[pairs:]
-    far_re = upper[:, :pairs] - lower[:, pairs : 2 * pairs]
-    far_im = upper[:, pairs : 2 * pairs] + lower[:, :pairs]
-    near = joined[:, 2 * pairs :]
-    near_re = near[:pairs, :settings] - near[pairs:, settings : 2 * settings]
-    near_im = near[:pairs, settings : 2 * settings] + near[pairs:, :settings]
-
-    onehot = lambda ids, size: (ids[:, None] == jnp.arange(size, dtype=jnp.int32)[None, :]).astype(jnp.float32)
-    front = onehot(setting[0] * settings + setting[1], pairs)
-    first = jnp.dot(amp_first, onehot(setting[0], settings).T, precision=HIGHEST)
-    first = jnp.where(section == 0, first, 0.0)
-    second = jnp.dot(amp_second, front.T, precision=HIGHEST)
-    third_pick = onehot(setting[2], settings)
-    fourth_pick = onehot(setting[2] * settings + setting[3], pairs)
-
-    def chosen(table, pick):
-        return jnp.sum(jnp.dot(front, table, precision=HIGHEST) * pick, axis=1)
-
-    third = jnp.stack([chosen(near_re, third_pick), chosen(near_im, third_pick)])
-    fourth = jnp.stack([chosen(far_re, fourth_pick), chosen(far_im, fourth_pick)])
-    partial = jnp.stack([first, second, third, fourth]).reshape(2 * sections, count)
-    summed = total(sections, ranks, partial).reshape(sections, 2, count)
+    unused = jnp.zeros((2 * (pairs - settings), 2 * count), jnp.float32)
+    nothing = jnp.zeros_like(amp)
+    summed = meet(
+        sections,
+        ranks,
+        u.reshape(sections * ranks, share, 2 * pairs),
+        w.reshape(sections, share, 4 * pairs),
+        twice(front),
+        twice(onehot(setting[2] * settings + setting[3], pairs)),
+        jnp.concatenate([twice(onehot(setting[2], settings)), unused]),
+        jnp.concatenate(
+            [jnp.where(section == 0, amp, 0.0), jnp.where(section == 1, amp, 0.0), nothing, nothing]
+        ),
+    ).reshape(sections, 2, count)
     own = lax.dynamic_index_in_dim(summed, section, 0, False)
     return own.reshape(1, 2, micro, batch)
 

time: 111 us -> 106 us (0.955)
  matrix products: 8.57 us -> 2.73 us
  local copies, waits for them, and re-layouts: 5.55 us -> 7.46 us
  Pallas kernels: 81.3 us -> 79.6 us
    dot_general x11 -> x2, matrix products: 7.13 us -> 1.28 us  [the longest x1 1.11 us: with_probe(): m = lax.dot_general(v, probe, (((1,), (1,)), ((), ())), precision=HIGHEST)]
    pallas_call x3 -> x2, Pallas kernels: 81.3 us -> 79.6 us  [call(): pl.pallas_call(kernel, out_shape=[jax.ShapeDtypeStruct(shape, jnp.float32...]
    unnamed x2, local copies, waits for them, and re-layouts: 0.01 us -> 1.33 us
where the time goes in v3:
time: 106 us; the launch traced here: 105 us
  Pallas kernels  79.6 us (75%)
  other arithmetic  15.4 us (15%)
  local copies, waits for them, and re-layouts  7.46 us (7%)
  matrix products  2.73 us (3%)
    pallas_call x2, Pallas kernels, call(): pl.pallas_call(kernel, out_shape=[jax.ShapeDtypeStruct(shape, jnp.float32...  79.6 us
    reduce_sum x1, other arithmetic, first_forward(): u_re = jnp.sum(b_re * t_re - b_im * t_im, axis=0)  12.2 us

profile of v3, /device:TPU:0, one launch (start us, length us, event | category | flops | bytes accessed | tf_op | source)
XLA Modules:
  0.0 105.4 jit_solution(3779172846378041691)
XLA Ops:
  0.1 0.8 fusion.76
  1.0 0.6 broadcast_in_dim.43.set_ref
  1.6 15.1 %conditional.2 = (f32[16,2048]{1,0:T(8,128)}) conditional(s32[]{:T(128)} %clamp.4, (s32[4,2048]{1,0:T(4,128)}, s32[]{:T(128)}, f32[2,2048]{1,0:T(2,128)}, f32[1,2,256,8,2048]{4,3,2,1,0:T(8,128)}) %tuple.41, () %tuple.42, () %tuple.43, (f32[1,2,256,8,2048]{4,3,2,1,0:T(8,128)}, f32[2,2048]{1,0:T(2,128)}, ...), branch_computations={%region_0.3_spmd, %region_3.4_spmd, %region_4.0_spmd, %region_5.8_... | conditional | flops 46661636 | bytes 33991736 | solution.py:271
  1.6 0.8 slice.103
  2.3 1.4 %fusion.5 = f32[2,256]{1,0:T(2,128)S(1)} fusion(f32[2,2048]{1,0:T(2,128)} %get-tuple-element.83, s32[256]{0:T(256)S(1)} %bitcast.165), kind=kOutput, calls=%fused_computation.10 | convolution fusion | flops 13107200 | bytes 19456 | tf_op jit(solution)/shard_map/cond/branch_0_fun/dot_general | solution.py:253
  3.8 12.2 %fusion.1 = (f32[8,2048]{1,0:T(8,128)S(1)}, f32[8,2048]{1,0:T(8,128)S(1)}) fusion(f32[1,2,256,8,2048]{4,3,2,1,0:T(8,128)} %get-tuple-element.55, f32[256]{0:T(256)S(1)} %bitcast.164, f32[256]{0:T(256)S(1)} %bitcast.163), kind=kLoop, calls=%fused_computation.3 | loop fusion | flops 33521664 | bytes 33687552 | tf_op jit(solution)/shard_map/cond/branch_0_fun/reduce_sum | solution.py:259
  16.0 0.7 pad_maximum_fusion
  16.7 1.6 %copy.45 = f32[2,8,8,256]{3,2,0,1:T(8,128)} copy(f32[2,8,8,256]{3,2,1,0:T(8,128)} %bitcast.45) | data formatting | bytes 262144 | tf_op jit(solution)/shard_map/reshape | solution.py:274
  18.2 16.6 %shard_map.56 = (f32[8,16,256]{2,1,0:T(8,128)}, f32[4,8,128]{2,1,0:T(8,128)}) custom-call(f32[8,16,256]{2,1,0:T(8,128)} %bitcast.149, f32[8,128]{1,0:T(8,128)} %broadcast_in_dim.43.set_ref), custom_call_target="tpu_custom_call" | custom-call | tf_op jit(solution)/shard_map/pallas_call | solution.py:45
  34.8 0.7 slice_convert_fusion
  35.5 0.9 copy.35
  36.5 0.7 concatenate.44.h_ref
  37.2 0.1 broadcast_multiply_fusion
  37.3 0.7 copy.43
  38.0 0.7 copy.44
  38.7 1.8 %conditional.3 = (f32[2,128]{1,0:T(2,128)S(1)}, f32[32,64,128]{2,1,0:T(8,128)S(1)}, f32[4,64,256]{2,1,0:T(8,128)S(1)}) conditional(s32[]{:T(128)} %clamp.4, (f32[16,2048]{1,0:T(8,128)}, f32[2,2048]{1,0:T(2,128)}, s32[4,1,128]{2,1,0:T(1,128)S(1)}) %tuple.81, (f32[16,2048]{1,0:T(8,128)S(1)}, s32[4,2048]{1,0:T(4,128)}, ...), branch_computations={%region_9.0_spmd, %region_10.11_spmd, %region_11.12_spmd, %region_... | conditional | flops 8878436352 | bytes 50216044 | solution.py:345
  38.7 1.1 %fusion.83 = f32[16,2]{0,1:T(2,128)S(1)} fusion(f32[16,2048]{1,0:T(8,128)} %get-tuple-element.59, f32[2,2048]{1,0:T(2,128)} %get-tuple-element.60), kind=kOutput, calls=%fused_computation.142 | convolution fusion | flops 786432 | bytes 147584 | tf_op jit(solution)/shard_map/cond/branch_0_fun/dot_general | solution.py:295
  39.8 0.1 subtract_bitcast_fusion
  39.9 0.2 fusion.11
  40.1 0.1 reshape.282
  40.5 0.7 maximum_maximum_fusion.e_ref
  41.1 63.0 %shard_map.57 = f32[8,128]{1,0:T(8,128)} custom-call(f32[32,64,128]{2,1,0:T(8,128)S(1)} %get-tuple-element.79.u_ref, f32[4,64,256]{2,1,0:T(8,128)S(1)} %get-tuple-element.80.w_ref, f32[128,256]{1,0:T(8,128)} %bitcast.151, f32[128,256]{1,0:T(8,128)} %bitcast.150, f32[128,256]{1,0:T(8,128)} %concatenate.44.h_ref, f32[8,128]{1,0:T(8,128)} %maximum_maximum_fusion.e_ref), custom_call_target="tpu_custom_call" | custom-call | tf_op jit(solution)/shard_map/pallas_call | solution.py:45
  104.1 0.6 constant_dynamic-slice_fusion.2
  104.8 0.7 reshape.300
  (15 shorter events, 0.3 us)
